TPU v7x, 256 devices: a whole 4x4x8 slice. The times are simulated.
256 devices in a mesh: grp: 32 (over y, z_lo, core), dev: 8 (over x, z_hi).
Axes of the slice: x: 4, y: 4, z: 8 (z_hi: 2, z_lo: 4; z = z_hi * 4 + z_lo), core: 2. Of those that a mesh axis runs over, the one named last changes fastest.
Arguments:
- stack: bfloat16 [608, 256, 2048], P('grp', None, 'dev'), may hold values from -12 to 12
- network: int32 [608, 2], replicated, may hold values from 0 to 149, as said below
- bands: int32 [149], replicated, may hold values from 1 to 8
Outputs:
- deramped: bfloat16 [149, 256, 2048], P(None, 'grp', 'dev')
- misfit: float32 [256, 2048], P('grp', 'dev')
- spectrum: float32 [2, 149, 15, 15], replicated
Inputs may be any that keep to these rules, and one draw needn't show every extreme that they name: `network`: each row holds a reference date and a later secondary date, both below 150; every pair of consecutive dates is some row.
All inputs are finite; a program needn't handle non-finite values.
Results may differ from a plain program's by a relative error of at most 0.005.
Values may be sent and summed in bfloat16 or wider, within the bound.
No kernel may reach another device: no remote copies, remote signals or barrier semaphores. Data moves between devices by JAX's collectives and lax.ppermute only.
A program may use at most 128 MiB of HBM per device.

v0:
```python
import math
import jax
import jax.numpy as jnp
import numpy as np
from jax import lax
from jax.sharding import PartitionSpec as P

BAND = 8
FREQS = 2 * BAND - 1
HIGH = lax.Precision.HIGHEST


def design_of(network, solved):
    dates = jnp.arange(1, solved + 1, dtype=jnp.int32)
    return (network[:, 1:2] == dates[None, :]).astype(jnp.float32) - (
        network[:, 0:1] == dates[None, :]
    ).astype(jnp.float32)


def build_inverse(network, solved):
    design = design_of(network, solved)
    normal = jnp.dot(design.T, design, precision=HIGH)
    factor = jnp.linalg.cholesky(normal)
    pinv = jax.scipy.linalg.cho_solve((factor, True), design.T)
    return (pinv.astype(jnp.bfloat16), design.astype(jnp.bfloat16))


def basis(positions, length):
    index = jnp.arange(FREQS, dtype=jnp.int32)
    step = jnp.where(index < BAND, index, index - (BAND - 1))
    turns = positions[:, None] * step[None, :] % length
    angle = turns.astype(jnp.float32) * (2.0 * math.pi / length)
    return jnp.where(index[None, :] < BAND, jnp.cos(angle), jnp.sin(angle))


def mirror():
    out = np.zeros((FREQS, FREQS, 2, FREQS, FREQS), np.float32)
    for k in range(FREQS):
        for l in range(FREQS):
            fk, fl = (k - (BAND - 1), l - (BAND - 1))
            ck, cl = (abs(fk), abs(fl))
            sk, sl = (abs(fk) + BAND - 1, abs(fl) + BAND - 1)
            gk, gl = (np.sign(fk), np.sign(fl))
            out[k, l, 0, ck, cl] += 1
            if gk * gl:
                out[k, l, 0, sk, sl] -= gk * gl
            if gk:
                out[k, l, 1, sk, cl] -= gk
            if gl:
                out[k, l, 1, ck, sl] -= gl
    return out.reshape(FREQS * FREQS * 2, FREQS * FREQS)


def on_device(stack, network, bands):
    solved = bands.shape[0]
    groups = lax.axis_size("grp")
    held, rows_all, col_dev = stack.shape
    row_dev = rows_all // groups
    cols_all = col_dev * lax.axis_size("dev")
    pixels = row_dev * col_dev
    packed = stack.reshape(held, groups, row_dev, col_dev).transpose(1, 0, 2, 3)
    block = lax.all_to_all(packed, "grp", 0, 0, tiled=True)
    rows = basis(jnp.arange(rows_all, dtype=jnp.int32), rows_all)
    cols = basis(lax.axis_index("dev") * col_dev + jnp.arange(col_dev, dtype=jnp.int32), cols_all)
    wide = stack.astype(jnp.float32)
    half = jnp.einsum("ihw,ha->iaw", wide, rows, precision=HIGH)
    local = jnp.einsum("iaw,wb->iab", half, cols, precision=HIGH)
    local = local.reshape(held, FREQS * FREQS)
    summed = lax.psum(local, "dev")
    every = lax.all_gather(summed, "grp", axis=0, tiled=True)
    pinv, design = build_inverse(network, solved)
    scale = 1.0 / (rows_all * cols_all)
    coef = scale * lax.dot_general(
        every, pinv.astype(jnp.float32), (((0,), (1,)), ((), ())), precision=HIGH
    )
    index = np.arange(FREQS)
    step = np.where(index < BAND, index, index - (BAND - 1))
    weight = np.where(step == 0, 1.0, 2.0)
    kmax = np.maximum(step[:, None], step[None, :]).reshape(-1)
    both = (weight[:, None] * weight[None, :]).reshape(-1).astype(np.float32)
    masked = jnp.where(jnp.asarray(kmax)[:, None] < bands[None, :], coef, 0.0)
    signed = jnp.dot(jnp.asarray(mirror()), masked, precision=HIGH)
    spectrum = signed.reshape(FREQS, FREQS, 2, solved).transpose(2, 3, 0, 1)
    row_here = basis(
        lax.axis_index("grp") * row_dev + jnp.arange(row_dev, dtype=jnp.int32), rows_all
    )
    waves = (row_here.T[:, None, :, None] * cols.T[None, :, None, :]).reshape(FREQS * FREQS, pixels)
    ramp = lax.dot_general(
        masked * jnp.asarray(both)[:, None], waves, (((0,), (0,)), ((), ())), precision=HIGH
    )
    flat = block.reshape(held * groups, pixels)
    series = jnp.dot(pinv, flat, preferred_element_type=jnp.float32)
    deramped = (series - ramp).astype(jnp.bfloat16).reshape(solved, row_dev, col_dev)
    model = jnp.dot(design, series.astype(jnp.bfloat16), preferred_element_type=jnp.float32)
    resid = flat.astype(jnp.float32) - model
    misfit = jnp.sqrt(jnp.mean(resid * resid, axis=0) + 1e-06).reshape(row_dev, col_dev)
    return (deramped, misfit, spectrum)


def solution(mesh):
    return jax.shard_map(
        on_device,
        mesh=mesh,
        in_specs=(P("grp", None, "dev"), P(), P()),
        out_specs=(P(None, "grp", "dev"), P("grp", "dev"), P()),
        check_vma=False,
    )
```

profile of v0, /device:TPU:1, one launch (start us, length us, event | category | flops | bytes accessed | tf_op | source)
XLA Modules:
  0.0 182.2 jit_solution(6894326143020125078)
XLA Ops:
  0.6 0.0 copy-start
  0.6 1.7 copy-done
  2.3 1.6 copy_bitcast_fusion
  4.0 10.4 %all-to-all-start = ((bf16[32,19,8,256]{3,2,1,0:T(8,128)(2,1)}), bf16[32,19,8,256]{3,2,1,0:T(8,128)(2,1)}, u32[]{:S(2)}, u32[]{:S(2)}) async-start(bf16[32,19,8,256]{3,2,1,0:T(8,128)(2,1)} %copy_bitcast_fusion), calls=%async_computation | async-start | bytes 4980736 | tf_op jit(solution)/shard_map/all_to_all | solution.py:62
  14.3 0.0 copy-done.9
  14.4 1.5 fusion.4
  15.9 0.1 copy.17
  16.1 11.7 %cholesky.51 = f32[128,128]{1,0:T(8,128)S(1)} custom-call(f32[128,128]{1,0:T(8,128)S(1)} %cholesky.124), custom_call_target="Cholesky" | custom-call | tf_op jit(solution)/shard_map/jit(cholesky)/cholesky | solution.py:23
  27.8 9.8 %custom-call.18 = f32[1,128,128]{1,2,0:T(8,128)S(1)} custom-call(f32[1,128,128]{2,1,0:T(8,128)S(1)} %get-tuple-element.26), custom_call_target="InvertDiagBlocksLowerTriangular" | custom-call | tf_op jit(solution)/shard_map/jit(cholesky)/cholesky | solution.py:23
  37.7 0.2 constant_dynamic-update-slice_fusion.1
  37.8 0.2 convolution_subtract_fusion.3
  38.0 1.9 %cholesky.110 = f32[21,21]{1,0:T(8,128)S(1)} custom-call(f32[21,21]{1,0:T(8,128)S(1)} %convolution_subtract_fusion.3), custom_call_target="Cholesky" | custom-call | tf_op jit(solution)/shard_map/jit(cholesky)/cholesky | solution.py:23
  39.9 0.6 compare_reduce_fusion
  40.6 0.6 compare_reduce_fusion.1
  42.5 0.0 copy-start.6
  42.6 0.1 fusion.20
  42.7 19.9 %custom-call.19 = f32[2,128,128]{1,2,0:T(8,128)S(1)} custom-call(f32[2,128,128]{2,1,0:T(8,128)S(1)} %pad_maximum_fusion.3), custom_call_target="InvertDiagBlocksLowerTriangular" | custom-call | tf_op jit(solution)/shard_map/jit(_cho_solve)/triangular_solve | solution.py:24
  62.6 0.0 copy-start.7
  62.6 0.1 convert_subtract_fusion.2
  62.7 0.7 fusion.7
  63.4 0.0 copy-start.2
  63.4 0.7 copy-done.2
  64.2 0.4 convolution_subtract_fusion.2
  64.6 0.3 fusion.53
  64.8 0.2 fusion.82
  65.0 0.2 copy.18
  65.3 0.0 copy-done.7
  65.3 1.2 convolution_bitcast_fusion
  66.5 0.0 copy-done.6
  66.5 0.5 fusion.32
  67.0 0.1 reshape.205
  67.1 45.8 %psum.7 = f32[19,225]{1,0:T(8,128)S(1)} all-reduce(f32[19,225]{1,0:T(8,128)S(1)} %reshape.205), channel_id=1, replica_groups=mesh['grp'=32,'dev'=8] {'dev'}, use_global_device_ids=true, to_apply=%region_4.5 | all-reduce | flops 4275 | bytes 34200 | tf_op jit(solution)/shard_map/psum | solution.py:69
  112.9 53.9 %all-gather = f32[32,19,225]{2,1,0:T(8,128)S(1)} all-gather(f32[1,19,225]{2,1,0:T(8,128)S(1)} %bitcast.72), channel_id=1, replica_groups=mesh['grp'=32,'dev'=8] {'grp'}, dimensions={0}, use_global_device_ids=true | all-gather | bytes 564300 | tf_op jit(solution)/shard_map/all_gather | solution.py:70
  166.8 0.9 reshape.238
  167.7 0.1 sine_select_fusion.1
  167.8 0.2 sine_select_fusion
  168.0 0.2 broadcast_multiply_fusion
  168.2 0.1 pad.23
  168.3 0.0 copy-start.3
  168.3 0.0 copy-start.8
  168.4 0.0 copy-start.4
  168.4 0.0 copy-start.11
  168.4 0.0 copy-start.12
  168.4 0.0 copy-start.5
  168.4 2.1 %copy.23 = f32[29,8,8,256]{3,1,2,0:T(8,128)} copy(f32[29,8,8,256]{3,2,1,0:T(8,128)S(1)} %bitcast.67) | data formatting | bytes 3801088
  170.5 0.0 copy-done.3
  170.5 1.4 convolution_subtract_fusion.1
  171.9 0.0 copy-done.8
  171.9 0.4 convolution_convert_fusion
  172.3 0.0 copy-done.4
  172.3 0.5 fusion.1
  172.9 0.5 fusion.83
  173.4 1.0 reshape.207
  174.5 0.0 all-to-all-done
  174.5 2.5 %copy.22 = bf16[76,8,8,256]{3,1,2,0:T(8,128)(2,1)S(1)} copy(bf16[76,8,8,256]{3,2,1,0:T(8,128)(2,1)} %bitcast.15) | data formatting | bytes 4980736
  177.0 0.7 fusion.16
  177.7 0.0 copy-start.10
  177.7 1.0 multiply_reduce_fusion
  178.7 0.5 copy-done.1
  179.2 0.0 copy-done.10
  179.2 1.3 fusion
  180.5 0.1 copy.24
  180.7 0.9 slice.94
  181.6 0.6 sqrt.8
  (22 shorter events, 0.2 us)
Async XLA Ops:
  0.6 1.7 copy-start
  4.0 10.4 %copy-start.9 = (s32[608,2]{0,1:T(2,128)S(1)}, s32[608,2]{0,1:T(2,128)}, u32[]{:S(2)}) copy-start(s32[608,2]{0,1:T(2,128)} %param.7) | copy-start | bytes 14596
  4.0 170.5 %all-to-all-start = ((bf16[32,19,8,256]{3,2,1,0:T(8,128)(2,1)}), bf16[32,19,8,256]{3,2,1,0:T(8,128)(2,1)}, u32[]{:S(2)}, u32[]{:S(2)}) async-start(bf16[32,19,8,256]{3,2,1,0:T(8,128)(2,1)} %copy_bitcast_fusion), calls=%async_computation | async-start | bytes 4980736 | tf_op jit(solution)/shard_map/all_to_all | solution.py:62
  42.5 23.9 %copy-start.6 = (f32[149,149]{1,0:T(8,128)}, f32[149,149]{1,0:T(8,128)S(1)}, u32[]{:S(2)}) copy-start(f32[149,149]{1,0:T(8,128)S(1)} %select_select_fusion) | copy-start | bytes 266416
  62.6 2.7 %copy-start.7 = (f32[2,128,128]{1,2,0:T(8,128)}, f32[2,128,128]{1,2,0:T(8,128)S(1)}, u32[]{:S(2)}) copy-start(f32[2,128,128]{1,2,0:T(8,128)S(1)} %custom-call.19) | copy-start | bytes 393220
  63.4 0.7 copy-start.2
  168.3 2.2 %copy-start.3 = (f32[128,608]{0,1:T(8,128)S(1)}, f32[128,608]{0,1:T(8,128)}, u32[]{:S(2)}) copy-start(f32[128,608]{0,1:T(8,128)} %copy-done.2) | copy-start | bytes 933892
  168.3 3.5 %copy-start.8 = (f32[2,128,128]{1,2,0:T(8,128)S(1)}, f32[2,128,128]{1,2,0:T(8,128)}, u32[]{:S(2)}) copy-start(f32[2,128,128]{1,2,0:T(8,128)} %copy-done.7) | copy-start | bytes 393220
  168.4 4.0 %copy-start.4 = (f32[608,225]{1,0:T(8,128)S(1)}, f32[608,225]{1,0:T(8,128)}, u32[]{:S(2)}) copy-start(f32[608,225]{1,0:T(8,128)} %reshape.238) | copy-start | bytes 1641604
  168.4 4.0 %copy-start.11 = (s32[149]{0:T(256)S(1)}, s32[149]{0:T(256)}, u32[]{:S(2)}) copy-start(s32[149]{0:T(256)} %param.8) | copy-start | bytes 1792
  168.4 4.0 %copy-start.12 = (s32[225]{0:T(256)S(1)}, s32[225]{0:T(256)}, u32[]{:S(2)}) copy-start(s32[225]{0:T(256)} %constant.175.clone) | copy-start | bytes 2704
  168.4 4.5 %copy-start.5 = (f32[450,225]{1,0:T(8,128)S(1)}, f32[450,225]{1,0:T(8,128)}, u32[]{:S(2)}) copy-start(f32[450,225]{1,0:T(8,128)} %constant.176.clone) | copy-start | bytes 1215004
  177.7 1.5 copy-start.1
  177.7 1.5 copy-start.10
where the time goes:
time: 183 us; the launch traced here: 182 us
  blocking collectives  99.7 us (54%)
  other arithmetic  45.4 us (25%)
  local copies, waits for them, and re-layouts  13.4 us (7%)
  matrix products  11 us (6%)
  starting transfers between devices  10.4 us (6%)
  between operations  2.38 us (1%)
    all_gather x1, blocking collectives, on_device(): every = lax.all_gather(summed, 'grp', axis=0, tiled=True)  53.9 us
    psum x1, blocking collectives, on_device(): summed = lax.psum(local, 'dev')  45.8 us
    another operation x7, other arithmetic, build_inverse(): factor = jnp.linalg.cholesky(normal)  24.8 us
    another operation x6, other arithmetic, build_inverse(): pinv = jax.scipy.linalg.cho_solve((factor, True), design.T)  20 us
    all_to_all x1, starting transfers between devices, on_device(): block = lax.all_to_all(packed, 'grp', 0, 0, tiled=True)  10.4 us
    unnamed x31, local copies, waits for them, and re-layouts  8.8 us
  transfers between devices with their start and end apart: 1, of which 0 were waited for; matrix products, arithmetic and copies ran while one was open for 32% of the time, Pallas kernels for 0%

commit v1 on v0

--- a/solution.py
+++ b/solution.py
@@ -67,7 +67,9 @@
     local = jnp.einsum("iaw,wb->iab", half, cols, precision=HIGH)
     local = local.reshape(held, FREQS * FREQS)
     summed = lax.psum(local, "dev")
-    every = lax.all_gather(summed, "grp", axis=0, tiled=True)
+    every = jnp.concatenate(
+        lax.all_to_all(jnp.stack([summed] * lax.axis_size("grp")), "grp", 0, 0), axis=0
+    )
     pinv, design = build_inverse(network, solved)
     scale = 1.0 / (rows_all * cols_all)
     coef = scale * lax.dot_general(

time: 183 us -> 170 us (0.929)
  blocking collectives: 99.7 us -> 49.3 us
  waiting for transfers between devices: 0.01 us -> 18.3 us
  starting transfers between devices: 10.4 us -> 18.7 us
  matrix products: 11 us -> 16 us
  other arithmetic: 45.4 us -> 48.4 us
  local copies, waits for them, and re-layouts: 13.4 us -> 16.2 us
    all_gather x1 -> x0, blocking collectives: 53.9 us -> none  [on_device(): every = lax.all_gather(summed, 'grp', axis=0, tiled=True)]
    all_to_all x0 -> x1, waiting for transfers between devices: none -> 18.3 us  [on_device(): lax.all_to_all(jnp.stack([summed] * lax.axis_size('grp')), 'grp', 0, 0)]
    all_to_all x0 -> x1, starting transfers between devices: none -> 13.9 us  [on_device(): lax.all_to_all(jnp.stack([summed] * lax.axis_size('grp')), 'grp', 0, 0)]
    all_to_all x1, starting transfers between devices: 10.4 us -> 4.76 us  [on_device(): block = lax.all_to_all(packed, 'grp', 0, 0, tiled=True)]
    psum x1, blocking collectives: 45.8 us -> 49.3 us  [on_device(): summed = lax.psum(local, 'dev')]
    unnamed x31 -> x36, local copies, waits for them, and re-layouts: 8.8 us -> 9.15 us
  transfers between devices with their start and end apart: 1 -> 2, of which waited for: 0 -> 1; matrix products, arithmetic and copies ran while one was open for 32% -> 39% of each run, Pallas kernels for 0% -> 0%
where the time goes in v1:
time: 170 us; the launch traced here: 169 us
  blocking collectives  49.3 us (29%)
  other arithmetic  48.4 us (28%)
  starting transfers between devices  18.7 us (11%)
  waiting for transfers between devices  18.3 us (11%)
  local copies, waits for them, and re-layouts  16.2 us (10%)
  matrix products  16 us (9%)
  between operations  2.36 us (1%)
    psum x1, blocking collectives, on_device(): summed = lax.psum(local, 'dev')  49.3 us
    another operation x7, other arithmetic, build_inverse(): factor = jnp.linalg.cholesky(normal)  25.4 us
    another operation x6, other arithmetic, build_inverse(): pinv = jax.scipy.linalg.cho_solve((factor, True), design.T)  20 us
    all_to_all x1, waiting for transfers between devices, on_device(): lax.all_to_all(jnp.stack([summed] * lax.axis_size('grp')), 'grp', 0, 0)  18.3 us
    all_to_all x1, starting transfers between devices, on_device(): lax.all_to_all(jnp.stack([summed] * lax.axis_size('grp')), 'grp', 0, 0)  13.9 us
    unnamed x36, local copies, waits for them, and re-layouts  9.15 us
    all_to_all x1, starting transfers between devices, on_device(): block = lax.all_to_all(packed, 'grp', 0, 0, tiled=True)  4.76 us
    another operation x6, matrix products, build_inverse(): pinv = jax.scipy.linalg.cho_solve((factor, True), design.T)  4.73 us
  transfers between devices with their start and end apart: 2, of which 1 were waited for; matrix products, arithmetic and copies ran while one was open for 39% of the time, Pallas kernels for 0%

profile of v1, /device:TPU:1, one launch (start us, length us, event | category | flops | bytes accessed | tf_op | source)
XLA Modules:
  0.0 169.3 jit_solution(4474578592433351477)
XLA Ops:
  0.6 0.0 copy-start
  0.7 1.7 copy-done
  2.3 1.2 convolution_bitcast_fusion
  3.5 0.5 fusion.32
  4.1 0.1 reshape.210
  4.2 49.3 %psum.7 = f32[19,225]{1,0:T(8,128)S(1)} all-reduce(f32[19,225]{1,0:T(8,128)S(1)} %reshape.210), channel_id=1, replica_groups=mesh['grp'=32,'dev'=8] {'dev'}, use_global_device_ids=true, to_apply=%region_4.5 | all-reduce | flops 4275 | bytes 34200 | tf_op jit(solution)/shard_map/psum | solution.py:69
  53.5 0.9 stack.2
  54.4 0.0 copy-done.10
  54.4 13.9 %all-to-all-start.1 = ((f32[32,19,225]{2,1,0:T(8,128)}), f32[32,19,225]{2,1,0:T(8,128)S(1)}, u32[]{:S(2)}, u32[]{:S(2)}) async-start(f32[32,19,225]{2,1,0:T(8,128)} %stack.2), calls=%async_computation.1 | async-start | bytes 1572864 | tf_op jit(solution)/shard_map/all_to_all | solution.py:71
  68.3 0.0 copy-start.12
  68.4 1.5 fusion.4
  69.9 0.8 copy.13
  70.7 1.6 copy_bitcast_fusion
  72.3 18.3 %all-to-all-done.1 = f32[32,19,225]{2,1,0:T(8,128)S(1)} async-done(((f32[32,19,225]{2,1,0:T(8,128)}), f32[32,19,225]{2,1,0:T(8,128)S(1)}, u32[]{:S(2)}, u32[]{:S(2)}) %all-to-all-start.1) | async-done | bytes 547232 | tf_op jit(solution)/shard_map/all_to_all | solution.py:71
  90.6 4.8 %all-to-all-start = ((bf16[32,19,8,256]{3,2,1,0:T(8,128)(2,1)}), bf16[32,19,8,256]{3,2,1,0:T(8,128)(2,1)}, u32[]{:S(2)}, u32[]{:S(2)}) async-start(bf16[32,19,8,256]{3,2,1,0:T(8,128)(2,1)} %copy_bitcast_fusion), calls=%async_computation | async-start | bytes 4980736 | tf_op jit(solution)/shard_map/all_to_all | solution.py:62
  95.4 0.9 fusion.17
  96.4 0.0 copy-start.6
  96.4 0.7 copy-done.6
  97.0 11.7 %cholesky.51 = f32[128,128]{1,0:T(8,128)S(1)} custom-call(f32[128,128]{1,0:T(8,128)S(1)} %cholesky.124), custom_call_target="Cholesky" | custom-call | tf_op jit(solution)/shard_map/jit(cholesky)/cholesky | solution.py:23
  108.8 10.4 %custom-call.18 = f32[1,128,128]{1,2,0:T(8,128)} custom-call(f32[1,128,128]{2,1,0:T(8,128)S(1)} %get-tuple-element.26), custom_call_target="InvertDiagBlocksLowerTriangular" | custom-call | tf_op jit(solution)/shard_map/jit(cholesky)/cholesky | solution.py:23
  119.2 1.0 constant_dynamic-update-slice_fusion.1
  120.3 0.9 convolution_subtract_fusion.3
  121.1 1.9 %cholesky.110 = f32[21,21]{1,0:T(8,128)S(1)} custom-call(f32[21,21]{1,0:T(8,128)S(1)} %convolution_subtract_fusion.3), custom_call_target="Cholesky" | custom-call | tf_op jit(solution)/shard_map/jit(cholesky)/cholesky | solution.py:23
  123.1 0.6 compare_reduce_fusion
  123.7 0.6 compare_reduce_fusion.1
  125.7 0.0 copy-start.5
  125.7 0.6 copy-done.5
  126.3 0.1 fusion.20
  126.5 19.9 %custom-call.19 = f32[2,128,128]{1,2,0:T(8,128)S(1)} custom-call(f32[2,128,128]{2,1,0:T(8,128)S(1)} %pad_maximum_fusion.3), custom_call_target="InvertDiagBlocksLowerTriangular" | custom-call | tf_op jit(solution)/shard_map/jit(_cho_solve)/triangular_solve | solution.py:24
  146.4 0.8 convert_subtract_fusion.2
  147.2 0.7 fusion.7
  147.9 0.0 copy-start.2
  147.9 0.7 copy-done.2
  148.6 1.1 convolution_subtract_fusion.2
  149.7 0.3 fusion.53
  150.0 0.2 fusion.82
  150.2 0.2 copy.14
  150.4 0.1 sine_select_fusion.1
  150.5 0.8 sine_select_fusion
  151.4 0.2 broadcast_multiply_fusion
  151.6 0.1 pad.23
  151.7 0.0 copy-start.3
  151.7 0.0 copy-start.8
  151.7 0.0 copy-start.14
  151.7 0.0 copy-start.15
  151.7 2.1 %copy.19 = f32[29,8,8,256]{3,1,2,0:T(8,128)} copy(f32[29,8,8,256]{3,2,1,0:T(8,128)S(1)} %bitcast.66) | data formatting | bytes 3801088
  153.8 1.4 convolution_subtract_fusion.1
  155.2 1.1 convolution_convert_fusion
  156.3 0.9 reshape.211
  157.3 1.6 fusion.1
  158.9 1.6 fusion.83
  160.5 1.0 reshape.213
  161.5 0.0 all-to-all-done
  161.5 2.6 %copy.18 = bf16[76,8,8,256]{3,1,2,0:T(8,128)(2,1)S(1)} copy(bf16[76,8,8,256]{3,2,1,0:T(8,128)(2,1)} %bitcast.14) | data formatting | bytes 4980736
  164.1 0.0 copy-start.13
  164.1 0.7 fusion.16
  164.8 0.0 copy-start.11
  164.8 1.0 multiply_reduce_fusion
  165.8 0.5 copy-done.1
  166.3 0.0 copy-done.11
  166.3 1.3 fusion
  167.6 0.1 copy.20
  167.8 0.9 slice.94
  168.7 0.6 sqrt.8
  (30 shorter events, 0.2 us)
Async XLA Ops:
  0.6 1.7 %copy-start = (bf16[19,256,256]{2,1,0:T(8,128)(2,1)S(1)}, bf16[19,256,256]{2,1,0:T(8,128)(2,1)}, u32[]{:S(2)}) copy-start(bf16[19,256,256]{2,1,0:T(8,128)(2,1)} %param.6) | copy-start | bytes 7471108
  2.3 52.1 %copy-start.10 = (s32[256]{0:T(256)}, s32[256]{0:T(256)S(1)}, u32[]{:S(2)}) copy-start(s32[256]{0:T(256)S(1)} %iota_add_fusion) | copy-start | bytes 3076
  2.3 66.0 %copy-start.9 = (s32[608,2]{0,1:T(2,128)S(1)}, s32[608,2]{0,1:T(2,128)}, u32[]{:S(2)}) copy-start(s32[608,2]{0,1:T(2,128)} %param.7) | copy-start | bytes 14596
  54.4 36.2 %all-to-all-start.1 = ((f32[32,19,225]{2,1,0:T(8,128)}), f32[32,19,225]{2,1,0:T(8,128)S(1)}, u32[]{:S(2)}, u32[]{:S(2)}) async-start(f32[32,19,225]{2,1,0:T(8,128)} %stack.2), calls=%async_computation.1 | async-start | bytes 1572864 | tf_op jit(solution)/shard_map/all_to_all | solution.py:71
  68.3 4.0 %copy-start.12 = (s32[149]{0:T(256)}, s32[149]{0:T(256)S(1)}, u32[]{:S(2)}) copy-start(s32[149]{0:T(256)S(1)} %iota_add_fusion.1) | copy-start | bytes 1792
  90.6 70.9 %all-to-all-start = ((bf16[32,19,8,256]{3,2,1,0:T(8,128)(2,1)}), bf16[32,19,8,256]{3,2,1,0:T(8,128)(2,1)}, u32[]{:S(2)}, u32[]{:S(2)}) async-start(bf16[32,19,8,256]{3,2,1,0:T(8,128)(2,1)} %copy_bitcast_fusion), calls=%async_computation | async-start | bytes 4980736 | tf_op jit(solution)/shard_map/all_to_all | solution.py:62
  96.4 0.7 copy-start.6
  125.7 0.7 copy-start.5
  146.4 3.9 %copy-start.7 = (f32[2,128,128]{1,2,0:T(8,128)}, f32[2,128,128]{1,2,0:T(8,128)S(1)}, u32[]{:S(2)}) copy-start(f32[2,128,128]{1,2,0:T(8,128)S(1)} %custom-call.19) | copy-start | bytes 393220
  147.9 0.7 copy-start.2
  151.7 2.1 %copy-start.3 = (f32[128,608]{0,1:T(8,128)S(1)}, f32[128,608]{0,1:T(8,128)}, u32[]{:S(2)}) copy-start(f32[128,608]{0,1:T(8,128)} %copy-done.2) | copy-start | bytes 933892
  151.7 3.5 %copy-start.8 = (f32[2,128,128]{1,2,0:T(8,128)S(1)}, f32[2,128,128]{1,2,0:T(8,128)}, u32[]{:S(2)}) copy-start(f32[2,128,128]{1,2,0:T(8,128)} %copy-done.7) | copy-start | bytes 393220
  151.7 5.5 %copy-start.14 = (s32[149]{0:T(256)S(1)}, s32[149]{0:T(256)}, u32[]{:S(2)}) copy-start(s32[149]{0:T(256)} %param.8) | copy-start | bytes 1792
  151.7 5.5 %copy-start.15 = (s32[225]{0:T(256)S(1)}, s32[225]{0:T(256)}, u32[]{:S(2)}) copy-start(s32[225]{0:T(256)} %constant.175.clone) | copy-start | bytes 2704
  161.5 2.6 %copy-start.4 = (bf16[128,608]{0,1:T(8,128)(2,1)S(1)}, bf16[128,608]{0,1:T(8,128)(2,1)}, u32[]{:S(2)}) copy-start(bf16[128,608]{0,1:T(8,128)(2,1)} %convolution_convert_fusion) | copy-start | bytes 466948
  164.1 0.7 copy-start.13
  164.8 1.5 copy-start.1
  164.8 1.5 copy-start.11
